TPU v7x, 32 devices: a whole 2x2x4 slice. The times are simulated.
32 devices in a mesh: replica: 8 (over z, core), tp: 4 (over y, x).
Axes of the slice: x: 2, y: 2, z: 4, core: 2. Of those that a mesh axis runs over, the one named last changes fastest.
Arguments:
- token_ids: int32 [128], replicated, may hold values from 0 to 8191
- embed_table: bfloat16 [8192, 8192], P('replica', 'tp'), may hold values from -6 to 6
- norm_gain: bfloat16 [8192], replicated, may hold values from 0.099609375 to 1.8984375
- w_query: bfloat16 [8192, 4096], P(('replica', 'tp')), may hold values from -0.0625 to 0.0625
- w_keyvalue: bfloat16 [8192, 2, 512], P(('replica', 'tp')), may hold values from -0.0625 to 0.0625
- key_cache: bfloat16 [512, 1024, 128], P(('replica', 'tp')), may hold values from -360 to 360
- value_cache: bfloat16 [512, 1024, 128], P(('replica', 'tp')), may hold values from -6 to 6
- cache_lengths: int32 [128], P('replica'), may hold values from 1 to 1024, as said below
Outputs:
- context: bfloat16 [512, 1024], P(('replica', 'tp'))
- query_weight_tp: bfloat16 [8192, 4096], P(None, 'tp')
- keyvalue_weight_tp: bfloat16 [8192, 2, 512], P(None, None, 'tp')
Inputs may be any that keep to these rules, and one draw needn't show every extreme that they name: `cache_lengths`: some sequence has exactly 1024 filled slots.
All inputs are finite; a program needn't handle non-finite values.
Results may differ from a plain program's by a relative error of at most 0.019.
The roundings to bfloat16 on the way count: a program that leaves them out, or rounds other values in their place, can miss the bound.
Values may be sent and summed in bfloat16 or wider, within the bound.
A program may use at most 128 MiB of HBM per device.

v0:
```python
import jax
import jax.numpy as jnp
from jax import lax
from jax.sharding import PartitionSpec as P


def attend(query, keys, values, key_new, value_new, lengths):
    scale = query.shape[-1] ** (-0.5)
    scores = jnp.einsum("rgd,rcd->rgc", query, keys, preferred_element_type=jnp.float32) * scale
    position = lax.broadcasted_iota(jnp.int32, scores.shape, 2)
    scores = jnp.where(position < lengths[:, None, None], scores, -jnp.inf)
    own = jnp.einsum("rgd,rd->rg", query, key_new, preferred_element_type=jnp.float32) * scale
    top = jnp.maximum(jnp.max(scores, axis=2), own)
    weights = jnp.exp(scores - top[:, :, None])
    own_weight = jnp.exp(own - top)
    total = jnp.sum(weights, axis=2) + own_weight
    weights = (weights / total[:, :, None]).astype(jnp.bfloat16)
    own_weight = (own_weight / total).astype(jnp.bfloat16)
    context = jnp.einsum("rgc,rcd->rgd", weights, values, preferred_element_type=jnp.float32)
    context = (
        context
        + own_weight.astype(jnp.float32)[:, :, None] * value_new.astype(jnp.float32)[:, None, :]
    )
    return context.astype(jnp.bfloat16)


def per_device(
    token_ids, embed_table, norm_gain, w_query, w_keyvalue, key_cache, value_cache, cache_lengths
):
    group_index = lax.axis_index("replica")
    tp_index = lax.axis_index("tp")
    vocab_rows, feature_cols = embed_table.shape
    batch = cache_lengths.shape[0]
    first_id = group_index * vocab_rows
    picked = token_ids - first_id
    columns = lax.broadcasted_iota(jnp.int32, (batch * lax.axis_size("replica"), vocab_rows), 1)
    onehot = (picked[:, None] == columns).astype(jnp.bfloat16)
    embedded = lax.psum_scatter(
        jnp.dot(onehot, embed_table, preferred_element_type=jnp.float32),
        "replica",
        scatter_dimension=0,
        tiled=True,
    ).astype(jnp.bfloat16)
    whole = lax.all_gather(embedded, "tp", axis=1, tiled=True)
    values32 = whole.astype(jnp.float32)
    mean_square = jnp.mean(values32 * values32, axis=1, keepdims=True)
    normed = (values32 * lax.rsqrt(mean_square + 1e-05) * norm_gain.astype(jnp.float32)).astype(
        jnp.bfloat16
    )
    width = normed.shape[1]
    query_rows = w_query.reshape(w_query.shape[0], 1, w_query.shape[1])
    query_mid, pair_mid = (
        lax.all_to_all(query_rows, "tp", split_axis=2, concat_axis=0, tiled=True),
        lax.all_to_all(w_keyvalue, "tp", split_axis=2, concat_axis=0, tiled=True),
    )
    flat_query = query_mid.reshape(query_mid.shape[0], query_mid.shape[2])
    pair_cols = pair_mid.shape[2]
    flat_pair = pair_mid.reshape(pair_mid.shape[0], 2 * pair_cols)
    query_full, pair_full = (
        lax.all_gather(flat_query, "replica", axis=0, tiled=True),
        lax.all_gather(flat_pair, "replica", axis=0, tiled=True),
    )
    query_acc = jnp.dot(normed, query_full, preferred_element_type=jnp.float32)
    pair_acc = jnp.dot(normed, pair_full, preferred_element_type=jnp.float32)
    query_local = query_acc.astype(jnp.bfloat16)
    pair_local = pair_acc.astype(jnp.bfloat16).reshape(batch, 2, pair_cols)
    query_heads, pair_heads = (
        lax.all_gather(query_local, "tp", axis=1, tiled=True),
        lax.all_gather(pair_local, "tp", axis=2, tiled=True),
    )
    head_size = key_cache.shape[2]
    kv_heads = pair_heads.shape[2] // head_size
    group = query_heads.shape[1] // (kv_heads * head_size)
    rows_here = key_cache.shape[0]
    first_row = tp_index * rows_here
    query_grouped = (
        query_heads.reshape(batch, kv_heads, group, head_size)
        .transpose(1, 0, 2, 3)
        .reshape(kv_heads * batch, group, head_size)
    )
    key_grouped = (
        pair_heads[:, 0]
        .reshape(batch, kv_heads, head_size)
        .transpose(1, 0, 2)
        .reshape(kv_heads * batch, head_size)
    )
    value_grouped = (
        pair_heads[:, 1]
        .reshape(batch, kv_heads, head_size)
        .transpose(1, 0, 2)
        .reshape(kv_heads * batch, head_size)
    )
    query_mine = lax.dynamic_slice_in_dim(query_grouped, first_row, rows_here, 0)
    key_mine = lax.dynamic_slice_in_dim(key_grouped, first_row, rows_here, 0)
    value_mine = lax.dynamic_slice_in_dim(value_grouped, first_row, rows_here, 0)
    sequence = (first_row + lax.broadcasted_iota(jnp.int32, (rows_here,), 0)) % batch
    matches = sequence[:, None] == lax.broadcasted_iota(jnp.int32, (rows_here, batch), 1)
    row_lengths = jnp.sum(jnp.where(matches, cache_lengths[None, :], 0), axis=1)
    context = attend(query_mine, key_cache, value_cache, key_mine, value_mine, row_lengths)
    context = context.reshape(rows_here, group * head_size)
    return (context, query_full, pair_full.reshape(width, 2, pair_cols))


def solution(mesh):
    return jax.shard_map(
        per_device,
        mesh=mesh,
        in_specs=(
            P(),
            P("replica", "tp"),
            P(),
            P(("replica", "tp"), None),
            P(("replica", "tp"), None, None),
            P(("replica", "tp"), None, None),
            P(("replica", "tp"), None, None),
            P("replica"),
        ),
        out_specs=(P(("replica", "tp"), None), P(None, "tp"), P(None, None, "tp")),
        check_vma=False,
    )
```

profile of v0, /device:TPU:0, one launch (start us, length us, event | category | flops | bytes accessed | tf_op | source)
XLA Modules:
  0.0 279.0 jit_solution(18418797829905342189)
XLA Ops:
  7.2 0.7 broadcast_subtract_fusion
  7.9 3.9 %fusion.6 = f32[128,2048]{1,0:T(8,128)} fusion(bf16[1024,2048]{1,0:T(8,128)(2,1)} %param.9, s32[128]{0:T(128)S(1)} %broadcast_subtract_fusion), kind=kOutput, calls=%fused_computation.17 | convolution fusion | flops 537001984 | bytes 5243392 | tf_op jit(solution)/shard_map/dot_general | solution.py:39
  11.9 0.0 all-gather.5.cloned.1.call-start
  11.9 1.0 copy.59
  12.9 13.5 %all_to_all.30 = bf16[256,2,512]{0,1,2:T(2,128)(2,1)S(1)} all-to-all(bf16[256,2,512]{0,1,2:T(2,128)(2,1)S(1)} %copy.59), channel_id=1, replica_groups=mesh['replica'=8,'tp'=4] {'tp'}, dimensions={2} | all-to-all | bytes 1048576 | tf_op jit(solution)/shard_map/all_to_all | solution.py:54
  26.5 0.6 copy.60
  27.1 0.9 copy.76
  28.0 0.0 all-gather.3.cloned.1.call-start
  28.1 7.1 %copy.56 = bf16[256,1,4096]{0,1,2:T(2,128)(2,1)} copy(bf16[256,1,4096]{2,0,1:T(8,128)(2,1)S(1)} %bitcast.52) | data formatting | bytes 4194304 | tf_op jit(solution)/shard_map/reshape | solution.py:51
  35.1 0.5 broadcast.60
  35.6 21.6 %reduce = bf16[4096,256]{1,0:T(8,128)(2,1)S(1)} reduce(bf16[4096,1,256]{2,1,0:T(2,128)(2,1)} %bitcast.48, bf16[]{:T(256)} %broadcast.60), dimensions={1}, to_apply=%bitcast.36.reduce_sub_computation | reduce | bytes 4194306
  57.2 2.1 reshape.81
  59.3 27.9 %all_to_all.31 = bf16[4,2,131072]{2,1,0:T(2,128)(2,1)S(1)} all-to-all(bf16[4,2,131072]{2,1,0:T(2,128)(2,1)} %reshape.81), channel_id=1, replica_groups=mesh['replica'=8,'tp'=4] {'tp'}, dimensions={0} | all-to-all | bytes 4194304 | tf_op jit(solution)/shard_map/all_to_all | solution.py:53
  87.1 3.3 %reshape.82 = bf16[4096,1,256]{2,1,0:T(2,128)(2,1)} reshape(bf16[4,2,131072]{2,1,0:T(2,128)(2,1)S(1)} %all_to_all.31) | data formatting | bytes 4194304
  90.4 2.6 copy.66
  93.0 2.4 copy.57
  95.5 0.2 select_reduce_fusion
  95.7 0.9 convert_element_type.34
  96.6 8.4 %all_gather.15 = bf16[16,8192]{1,0:T(8,128)(2,1)S(1)} all-gather(bf16[16,2048]{1,0:T(8,128)(2,1)S(1)} %convert_element_type.34), channel_id=1, replica_groups=mesh['replica'=8,'tp'=4] {'tp'}, dimensions={1}, use_global_device_ids=true | all-gather | bytes 327680 | tf_op jit(solution)/shard_map/all_gather | solution.py:44
  105.0 0.2 fusion.3
  105.2 3.8 %fusion.2 = bf16[2,2,8,128]{3,2,1,0:T(8,128)(2,1)S(1)} fusion(bf16[8192,256]{1,0:T(8,128)(2,1)} %all-gather.5.cloned.1.call-done, bf16[16,8192]{1,0:T(8,128)(2,1)S(1)} %all_gather.15, f32[8192]{0:T(1024)S(1)} %convert_element_type.36, f32[16]{0:T(128)S(1)} %add_rsqrt_fusion), kind=kOutput, calls=%fused_computation.6 | convolution fusion | flops 67637248 | bytes 4497472 | tf_op jit(solution)/shard_map/dot_general | solution.py:64
  109.0 7.4 %all_gather.19 = bf16[16,2,512]{2,0,1:T(8,128)(2,1)S(1)} all-gather(bf16[16,2,128]{2,0,1:T(8,128)(2,1)S(1)} %bitcast.65), channel_id=1, replica_groups=mesh['replica'=8,'tp'=4] {'tp'}, dimensions={2}, use_global_device_ids=true | all-gather | bytes 40960 | tf_op jit(solution)/shard_map/all_gather | solution.py:69
  116.5 7.0 %reshape.78 = bf16[8192,2,128]{2,1,0:T(2,128)(2,1)} reshape(bf16[8192,256]{1,0:T(8,128)(2,1)} %all-gather.5.cloned.1.call-done) | data formatting | bytes 8388608 | tf_op jit(solution)/shard_map/reshape | solution.py:101
  123.5 122.8 %all-gather.3.cloned.1.call-done = bf16[8192,1024]{1,0:T(8,128)(2,1)} async-done(((bf16[1024,1024]{1,0:T(8,128)(2,1)}), bf16[8192,1024]{1,0:T(8,128)(2,1)}) %all-gather.3.cloned.1.call-update) | async-done | bytes 16777232 | tf_op jit(solution)/shard_map/all_gather | solution.py:60
  246.3 8.2 %convolution_convert_fusion = bf16[16,1024]{1,0:T(8,128)(2,1)S(1)} fusion(bf16[8192,1024]{1,0:T(8,128)(2,1)} %all-gather.3.cloned.1.call-done, bf16[16,8192]{1,0:T(8,128)(2,1)S(1)} %all_gather.15, f32[8192]{0:T(1024)S(1)} %convert_element_type.36, f32[16]{0:T(128)S(1)} %add_rsqrt_fusion), kind=kOutput, calls=%fused_computation.4 | convolution fusion | flops 268976128 | bytes 17104960 | tf_op jit(solution)/shard_map/dot_general | solution.py:63
  254.5 8.7 %all_gather.17 = bf16[16,4096]{1,0:T(8,128)(2,1)S(1)} all-gather(bf16[16,1024]{1,0:T(8,128)(2,1)S(1)} %convolution_convert_fusion), channel_id=1, replica_groups=mesh['replica'=8,'tp'=4] {'tp'}, dimensions={1}, use_global_device_ids=true | all-gather | bytes 163840 | tf_op jit(solution)/shard_map/all_gather | solution.py:68
  263.3 0.1 fusion.13
  263.4 1.3 fusion.23
  264.7 0.2 fusion.7
  265.0 0.7 fusion.1
  265.7 0.6 copy.77
  266.3 6.2 %copy.80 = bf16[8192,1024]{1,0:T(8,128)(2,1)} copy(bf16[8192,1024]{1,0:T(8,128)(2,1)S(1)} %bitcast.47) | data formatting | bytes 33554432
  (42 shorter events, 0.3 us)
Async XLA Ops:
  7.2 4.8 %copy-start.3 = (bf16[256,2,512]{2,1,0:T(2,128)(2,1)S(1)}, bf16[256,2,512]{2,1,0:T(2,128)(2,1)}, u32[]{:S(2)}) copy-start(bf16[256,2,512]{2,1,0:T(2,128)(2,1)} %param.12) | copy-start | bytes 1572868
  7.2 88.5 %reduce-scatter.2.cloned.1.call-start = ((), (), s32[]{:S(2)}) async-start(), calls=%async_computation.3 | async-start | bytes 1179648 | tf_op jit(solution)/shard_map/reduce_scatter | solution.py:38
  11.8 16.2 %copy-start.2 = (bf16[256,4096]{1,0:T(8,128)(2,1)S(1)}, bf16[256,4096]{1,0:T(8,128)(2,1)}, u32[]{:S(2)}) copy-start(bf16[256,4096]{1,0:T(8,128)(2,1)} %param.11) | copy-start | bytes 6291460
  11.9 93.3 %all-gather.5.cloned.1.call-start = ((), (), s32[]{:S(2)}) async-start(), calls=%async_computation.5 | async-start | bytes 4718592 | tf_op jit(solution)/shard_map/all_gather | solution.py:61
  28.0 218.3 %all-gather.3.cloned.1.call-start = ((), (), s32[]{:S(2)}) async-start(), calls=%async_computation.4 | async-start | bytes 18874368 | tf_op jit(solution)/shard_map/all_gather | solution.py:60
  93.0 2.4 copy-start.4
  93.0 2.5 copy-start.5
  246.3 17.1 %copy-start.1 = (bf16[16,1024,128]{2,1,0:T(8,128)(2,1)S(1)}, bf16[16,1024,128]{2,1,0:T(8,128)(2,1)}, u32[]{:S(2)}) copy-start(bf16[16,1024,128]{2,1,0:T(8,128)(2,1)} %param.13) | copy-start | bytes 12582916
  246.3 20.0 %slice-start = ((s8[16777216]{0:T(1024)(128)(4,1)}), s8[4194304]{0:T(1024)(128)(4,1)S(1)}, s32[]{:S(2)}) async-start(s8[16777216]{0:T(1024)(128)(4,1)} %bitcast.46), calls=%async_computation.6 | async-start | bytes 8388608
  246.3 20.0 %slice-start.1 = ((s8[16777216]{0:T(1024)(128)(4,1)}), s8[4194304]{0:T(1024)(128)(4,1)S(1)}, s32[]{:S(2)}) async-start(s8[16777216]{0:T(1024)(128)(4,1)} %bitcast.46), calls=%async_computation.7 | async-start | bytes 8388608
  246.3 20.0 %slice-start.2 = ((s8[16777216]{0:T(1024)(128)(4,1)}), s8[4194304]{0:T(1024)(128)(4,1)S(1)}, s32[]{:S(2)}) async-start(s8[16777216]{0:T(1024)(128)(4,1)} %bitcast.46), calls=%async_computation.8 | async-start | bytes 8388608
  254.5 10.4 %copy-start = (bf16[16,1024,128]{2,1,0:T(8,128)(2,1)S(1)}, bf16[16,1024,128]{2,1,0:T(8,128)(2,1)}, u32[]{:S(2)}) copy-start(bf16[16,1024,128]{2,1,0:T(8,128)(2,1)} %param.14) | copy-start | bytes 12582916
  263.4 2.9 %slice-start.3 = ((s8[16777216]{0:T(1024)(128)(4,1)}), s8[4194304]{0:T(1024)(128)(4,1)S(1)}, s32[]{:S(2)}) async-start(s8[16777216]{0:T(1024)(128)(4,1)} %bitcast.46), calls=%async_computation.9 | async-start | bytes 8388608
Sparse Core Ops, SparseCore 0:
  12.0 35.2 reduce-scatter.1
  48.9 45.1 all-gather.4
  96.4 149.8 all-gather.2
where the time goes:
time: 280 us; the launch traced here: 279 us
  waiting for transfers between devices  123 us (44%)
  blocking collectives  65.9 us (24%)
  local copies, waits for them, and re-layouts  34.3 us (12%)
  other arithmetic  23.9 us (9%)
  matrix products  18 us (6%)
  between operations  14 us (5%)
    all_gather x1, waiting for transfers between devices, per_device(): lax.all_gather(flat_query, 'replica', axis=0, tiled=True)  123 us
    all_to_all x1, blocking collectives, per_device(): lax.all_to_all(query_rows, 'tp', split_axis=2, concat_axis=0, tiled=True)  27.9 us
    unnamed x2, other arithmetic  21.6 us
    unnamed x29, local copies, waits for them, and re-layouts  17.2 us
    all_to_all x1, blocking collectives, per_device(): lax.all_to_all(w_keyvalue, 'tp', split_axis=2, concat_axis=0, tiled=True)  13.5 us
    all_gather x1, blocking collectives, per_device(): lax.all_gather(query_local, 'tp', axis=1, tiled=True)  8.68 us
    all_gather x1, blocking collectives, per_device(): whole = lax.all_gather(embedded, 'tp', axis=1, tiled=True)  8.37 us
    dot_general x1, matrix products, per_device(): query_acc = jnp.dot(normed, query_full, preferred_element_type=jnp.float32)  8.22 us
  transfers between devices with their start and end apart: 3, of which 1 were waited for; matrix products, arithmetic and copies ran while one was open for 19% of the time, Pallas kernels for 0%

commit v1 on v0

--- a/solution.py
+++ b/solution.py
@@ -50,7 +50,12 @@
     width = normed.shape[1]
     query_rows = w_query.reshape(w_query.shape[0], 1, w_query.shape[1])
     query_mid, pair_mid = (
-        lax.all_to_all(query_rows, "tp", split_axis=2, concat_axis=0, tiled=True),
+        jnp.concatenate(
+            lax.all_to_all(
+                jnp.stack(jnp.split(query_rows, lax.axis_size("tp"), axis=2)), "tp", 0, 0
+            ),
+            axis=0,
+        ),
         lax.all_to_all(w_keyvalue, "tp", split_axis=2, concat_axis=0, tiled=True),
     )
     flat_query = query_mid.reshape(query_mid.shape[0], query_mid.shape[2])

time: 280 us -> 280 us (level)
  waiting for transfers between devices: 123 us -> 163 us
  other arithmetic: 23.9 us -> 2.55 us
  local copies, waits for them, and re-layouts: 34.3 us -> 16.6 us
    all_gather x1, waiting for transfers between devices: 0.02 us -> 28.9 us  [per_device(): lax.all_gather(flat_pair, 'replica', axis=0, tiled=True)]
    unnamed x2 -> x1, other arithmetic: 21.6 us -> 0.01 us
    all_gather x1, waiting for transfers between devices: 123 us -> 133 us  [per_device(): lax.all_gather(flat_query, 'replica', axis=0, tiled=True)]
    unnamed x29 -> x25, local copies, waits for them, and re-layouts: 17.2 us -> 8.73 us
    reshape x1 -> x0, local copies, waits for them, and re-layouts: 7.06 us -> none  [per_device(): query_rows = w_query.reshape(w_query.shape[0], 1, w_query.shape[1])]
  transfers between devices with their start and end apart: 3 -> 3, of which waited for: 1 -> 2; matrix products, arithmetic and copies ran while one was open for 19% -> 5% of each run, Pallas kernels for 0% -> 0%
where the time goes in v1:
time: 280 us; the launch traced here: 279 us
  waiting for transfers between devices  163 us (58%)
  blocking collectives  66.1 us (24%)
  matrix products  17.2 us (6%)
  local copies, waits for them, and re-layouts  16.6 us (6%)
  between operations  14 us (5%)
    all_gather x1, waiting for transfers between devices, per_device(): lax.all_gather(flat_query, 'replica', axis=0, tiled=True)  133 us
    all_gather x1, waiting for transfers between devices, per_device(): lax.all_gather(flat_pair, 'replica', axis=0, tiled=True)  28.9 us
    all_to_all x1, blocking collectives, per_device(): lax.all_to_all(jnp.stack(jnp.split(query_rows, lax.axis_size('tp'), axis=...  27.5 us
    all_to_all x1, blocking collectives, per_device(): lax.all_to_all(w_keyvalue, 'tp', split_axis=2, concat_axis=0, tiled=True)  13.5 us
    unnamed x25, local copies, waits for them, and re-layouts  8.73 us
    all_gather x1, blocking collectives, per_device(): lax.all_gather(query_local, 'tp', axis=1, tiled=True)  8.68 us
    all_gather x1, blocking collectives, per_device(): whole = lax.all_gather(embedded, 'tp', axis=1, tiled=True)  8.38 us
    dot_general x1, matrix products, per_device(): query_acc = jnp.dot(normed, query_full, preferred_element_type=jnp.float32)  8.22 us
  transfers between devices with their start and end apart: 3, of which 2 were waited for; matrix products, arithmetic and copies ran while one was open for 5% of the time, Pallas kernels for 0%

profile of v1, /device:TPU:0, one launch (start us, length us, event | category | flops | bytes accessed | tf_op | source)
XLA Modules:
  0.0 279.0 jit_solution(6646729180478213800)
XLA Ops:
  7.2 0.0 reduce-scatter.2.cloned.1.call-start
  7.2 0.7 broadcast_subtract_fusion
  7.9 3.9 %fusion.6 = f32[128,2048]{1,0:T(8,128)} fusion(bf16[1024,2048]{1,0:T(8,128)(2,1)} %param.9, s32[128]{0:T(128)S(1)} %broadcast_subtract_fusion), kind=kOutput, calls=%fused_computation.22 | convolution fusion | flops 537001984 | bytes 5243392 | tf_op jit(solution)/shard_map/dot_general | solution.py:39
  11.9 0.0 reduce-scatter.2.cloned.1.call-update
  11.9 0.0 all-gather.5.cloned.1.call-start
  11.9 1.0 copy.41
  12.9 13.5 %all_to_all.20 = bf16[256,2,512]{0,1,2:T(2,128)(2,1)S(1)} all-to-all(bf16[256,2,512]{0,1,2:T(2,128)(2,1)S(1)} %copy.41), channel_id=1, replica_groups=mesh['replica'=8,'tp'=4] {'tp'}, dimensions={2} | all-to-all | bytes 1048576 | tf_op jit(solution)/shard_map/all_to_all | solution.py:59
  26.5 0.6 copy.42
  27.1 0.9 copy.57
  28.0 0.0 all-gather.5.cloned.1.call-update
  28.0 0.0 all-gather.3.cloned.1.call-start
  28.0 0.2 slice_bitcast_fusion.3
  28.2 0.3 pad_maximum_fusion
  28.5 27.5 %all_to_all.21 = bf16[4,256,1,1024]{3,1,2,0:T(8,128)(2,1)} all-to-all(bf16[4,256,1,1024]{3,1,2,0:T(8,128)(2,1)S(1)} %pad_maximum_fusion), channel_id=1, replica_groups=mesh['replica'=8,'tp'=4] {'tp'}, dimensions={0} | all-to-all | bytes 4194304 | tf_op jit(solution)/shard_map/all_to_all | solution.py:54
  56.0 0.0 all-gather.3.cloned.1.call-update
  56.1 0.2 select_reduce_fusion
  56.3 0.9 convert_element_type.34
  57.2 8.4 %all_gather.15 = bf16[16,8192]{1,0:T(8,128)(2,1)S(1)} all-gather(bf16[16,2048]{1,0:T(8,128)(2,1)S(1)} %convert_element_type.34), channel_id=1, replica_groups=mesh['replica'=8,'tp'=4] {'tp'}, dimensions={1}, use_global_device_ids=true | all-gather | bytes 327680 | tf_op jit(solution)/shard_map/all_gather | solution.py:44
  65.6 0.2 fusion.3
  65.8 28.9 %all-gather.5.cloned.1.call-done = bf16[8192,256]{1,0:T(8,128)(2,1)} async-done(((bf16[1024,256]{1,0:T(8,128)(2,1)}), bf16[8192,256]{1,0:T(8,128)(2,1)}) %all-gather.5.cloned.1.call-update) | async-done | bytes 4194320 | tf_op jit(solution)/shard_map/all_gather | solution.py:66
  94.8 2.9 %fusion.2 = bf16[2,2,8,128]{3,2,1,0:T(8,128)(2,1)S(1)} fusion(bf16[8192,256]{1,0:T(8,128)(2,1)} %all-gather.5.cloned.1.call-done, bf16[16,8192]{1,0:T(8,128)(2,1)S(1)} %all_gather.15, f32[8192]{0:T(1024)S(1)} %convert_element_type.36, f32[16]{0:T(128)S(1)} %add_rsqrt_fusion), kind=kOutput, calls=%fused_computation.7 | convolution fusion | flops 67637248 | bytes 4497472 | tf_op jit(solution)/shard_map/dot_general | solution.py:69
  97.7 8.0 %all_gather.19 = bf16[16,2,512]{2,0,1:T(8,128)(2,1)S(1)} all-gather(bf16[16,2,128]{2,0,1:T(8,128)(2,1)S(1)} %bitcast.65), channel_id=1, replica_groups=mesh['replica'=8,'tp'=4] {'tp'}, dimensions={2}, use_global_device_ids=true | all-gather | bytes 40960 | tf_op jit(solution)/shard_map/all_gather | solution.py:74
  105.7 7.1 %reshape.73 = bf16[8192,2,128]{2,1,0:T(2,128)(2,1)} reshape(bf16[8192,256]{1,0:T(8,128)(2,1)} %all-gather.5.cloned.1.call-done) | data formatting | bytes 8388608 | tf_op jit(solution)/shard_map/reshape | solution.py:106
  112.8 133.5 %all-gather.3.cloned.1.call-done = bf16[8192,1024]{1,0:T(8,128)(2,1)} async-done(((bf16[1024,1024]{1,0:T(8,128)(2,1)}), bf16[8192,1024]{1,0:T(8,128)(2,1)}) %all-gather.3.cloned.1.call-update) | async-done | bytes 16777232 | tf_op jit(solution)/shard_map/all_gather | solution.py:65
  246.3 8.2 %convolution_convert_fusion = bf16[16,1024]{1,0:T(8,128)(2,1)S(1)} fusion(bf16[8192,1024]{1,0:T(8,128)(2,1)} %all-gather.3.cloned.1.call-done, bf16[16,8192]{1,0:T(8,128)(2,1)S(1)} %all_gather.15, f32[8192]{0:T(1024)S(1)} %convert_element_type.36, f32[16]{0:T(128)S(1)} %add_rsqrt_fusion), kind=kOutput, calls=%fused_computation.5 | convolution fusion | flops 268976128 | bytes 17104960 | tf_op jit(solution)/shard_map/dot_general | solution.py:68
  254.5 8.7 %all_gather.17 = bf16[16,4096]{1,0:T(8,128)(2,1)S(1)} all-gather(bf16[16,1024]{1,0:T(8,128)(2,1)S(1)} %convolution_convert_fusion), channel_id=1, replica_groups=mesh['replica'=8,'tp'=4] {'tp'}, dimensions={1}, use_global_device_ids=true | all-gather | bytes 163840 | tf_op jit(solution)/shard_map/all_gather | solution.py:73
  263.3 0.1 fusion.13
  263.4 1.3 fusion.23
  264.7 0.2 fusion.7
  265.0 0.7 fusion.1
  265.7 0.6 copy.58
  266.3 6.2 %copy.61 = bf16[8192,1024]{1,0:T(8,128)(2,1)} copy(bf16[8192,1024]{1,0:T(8,128)(2,1)S(1)} %bitcast.50) | data formatting | bytes 33554432
  (37 shorter events, 0.2 us)
Async XLA Ops:
  7.2 4.8 %copy-start.3 = (bf16[256,2,512]{2,1,0:T(2,128)(2,1)S(1)}, bf16[256,2,512]{2,1,0:T(2,128)(2,1)}, u32[]{:S(2)}) copy-start(bf16[256,2,512]{2,1,0:T(2,128)(2,1)} %param.12) | copy-start | bytes 1572868
  7.2 49.1 %reduce-scatter.2.cloned.1.call-start = ((), (), s32[]{:S(2)}) async-start(), calls=%async_computation.3 | async-start | bytes 1179648 | tf_op jit(solution)/shard_map/reduce_scatter | solution.py:38
  11.9 16.2 %copy-start.2 = (bf16[256,4096]{1,0:T(8,128)(2,1)S(1)}, bf16[256,4096]{1,0:T(8,128)(2,1)}, u32[]{:S(2)}) copy-start(bf16[256,4096]{1,0:T(8,128)(2,1)} %param.11) | copy-start | bytes 6291460
  11.9 82.9 %all-gather.5.cloned.1.call-start = ((), (), s32[]{:S(2)}) async-start(), calls=%async_computation.5 | async-start | bytes 4718592 | tf_op jit(solution)/shard_map/all_gather | solution.py:66
  28.0 218.3 %all-gather.3.cloned.1.call-start = ((), (), s32[]{:S(2)}) async-start(), calls=%async_computation.4 | async-start | bytes 18874368 | tf_op jit(solution)/shard_map/all_gather | solution.py:65
  28.5 27.6 %copy-start.4 = (bf16[8192]{0:T(1024)(128)(2,1)S(1)}, bf16[8192]{0:T(1024)(128)(2,1)}, u32[]{:S(2)}) copy-start(bf16[8192]{0:T(1024)(128)(2,1)} %param.10) | copy-start | bytes 49156
  28.5 27.6 %copy-start.5 = (s32[16]{0:T(128)S(1)}, s32[16]{0:T(128)}, u32[]{:S(2)}) copy-start(s32[16]{0:T(128)} %param.15) | copy-start | bytes 196
  246.3 17.1 %copy-start.1 = (bf16[16,1024,128]{2,1,0:T(8,128)(2,1)S(1)}, bf16[16,1024,128]{2,1,0:T(8,128)(2,1)}, u32[]{:S(2)}) copy-start(bf16[16,1024,128]{2,1,0:T(8,128)(2,1)} %param.13) | copy-start | bytes 12582916
  246.3 20.0 %slice-start = ((s8[16777216]{0:T(1024)(128)(4,1)}), s8[4194304]{0:T(1024)(128)(4,1)S(1)}, s32[]{:S(2)}) async-start(s8[16777216]{0:T(1024)(128)(4,1)} %bitcast.49), calls=%async_computation.6 | async-start | bytes 8388608
  246.3 20.0 %slice-start.1 = ((s8[16777216]{0:T(1024)(128)(4,1)}), s8[4194304]{0:T(1024)(128)(4,1)S(1)}, s32[]{:S(2)}) async-start(s8[16777216]{0:T(1024)(128)(4,1)} %bitcast.49), calls=%async_computation.7 | async-start | bytes 8388608
  246.3 20.0 %slice-start.2 = ((s8[16777216]{0:T(1024)(128)(4,1)}), s8[4194304]{0:T(1024)(128)(4,1)S(1)}, s32[]{:S(2)}) async-start(s8[16777216]{0:T(1024)(128)(4,1)} %bitcast.49), calls=%async_computation.8 | async-start | bytes 8388608
  254.5 10.4 %copy-start = (bf16[16,1024,128]{2,1,0:T(8,128)(2,1)S(1)}, bf16[16,1024,128]{2,1,0:T(8,128)(2,1)}, u32[]{:S(2)}) copy-start(bf16[16,1024,128]{2,1,0:T(8,128)(2,1)} %param.14) | copy-start | bytes 12582916
  263.4 2.9 %slice-start.3 = ((s8[16777216]{0:T(1024)(128)(4,1)}), s8[4194304]{0:T(1024)(128)(4,1)S(1)}, s32[]{:S(2)}) async-start(s8[16777216]{0:T(1024)(128)(4,1)} %bitcast.49), calls=%async_computation.9 | async-start | bytes 8388608
Sparse Core Ops, SparseCore 0:
  12.0 35.2 reduce-scatter.1
  49.5 45.1 all-gather.4
  96.4 149.8 all-gather.2
